TPU v7x, 8 devices: a whole 2x2x1 slice. The times are simulated.
8 devices in a mesh: dp: 1 (over z), tp: 2 (over y), ep: 4 (over x, core).
Axes of the slice: x: 2, y: 2, z: 1, core: 2. Of those that a mesh axis runs over, the one named last changes fastest.
Arguments:
- x_in: bfloat16 [4096, 1024], P(('dp', 'ep', 'tp'))
- norm_gain: bfloat16 [1024], replicated
- w_router: bfloat16 [1024, 32], replicated
- expert_idx: int32 [4096, 8], P(('dp', 'ep', 'tp'))
- w_gate: bfloat16 [32, 1024, 512], P('ep', None, 'tp')
- w_up: bfloat16 [32, 1024, 512], P('ep', None, 'tp')
- w_down: bfloat16 [32, 512, 1024], P('ep', 'tp')
- out_bias: bfloat16 [1024], replicated
- dy_out: bfloat16 [4096, 1024], P(('dp', 'ep', 'tp'))
Outputs:
- output 1: bfloat16 [4096, 1024], P(('dp', 'ep', 'tp'))
- output 2: bfloat16 [4096, 1024], P(('dp', 'ep', 'tp'))
- output 3: float32 [1024], P('dp')
- output 4: float32 [1024, 32], P('dp')
- output 5: float32 [32, 1024, 512], P(('dp', 'ep'), None, 'tp')
- output 6: float32 [32, 1024, 512], P(('dp', 'ep'), None, 'tp')
- output 7: float32 [32, 512, 1024], P(('dp', 'ep'), 'tp')
- output 8: float32 [1024], P('dp')
All inputs are finite; a program needn't handle non-finite values.
Results may differ from a plain program's by a relative error of at most 0.0127574.
Values are sent between devices in bfloat16 or wider.
A program may use at most 1 GiB of HBM per device.

v0:
```python
import jax
import jax.numpy as jnp
from jax import lax
from jax.sharding import PartitionSpec as P

EPS = 1e-6


def routing_tables(expert_ids, n_exp, capacity):
    n_tok, top_k = expert_ids.shape
    flat_ids = expert_ids.reshape(-1)
    order = jnp.argsort(flat_ids, stable=True)
    counts = jnp.sum((flat_ids[:, None] == jnp.arange(n_exp)[None, :]).astype(jnp.int32), axis=0)
    starts = jnp.cumsum(counts) - counts
    slot_rank = jnp.arange(capacity)[None, :]
    slot_copy = order[jnp.minimum(starts[:, None] + slot_rank, n_tok * top_k - 1)]
    slot_ok = slot_rank < counts[:, None]
    copy_pos = flat_ids * capacity + jnp.argsort(order) - starts[flat_ids]
    return slot_copy, slot_ok, copy_pos.reshape(n_tok, top_k)


def solution(mesh):
    tok_spec = P(("dp", "ep", "tp"), None)
    wide_spec = P("ep", None, "tp")
    down_spec = P("ep", "tp", None)
    grad_wide = P(("dp", "ep"), None, "tp")
    grad_down = P(("dp", "ep"), "tp", None)

    def device_step(x_in, norm_gain, w_router, expert_idx, w_gate, w_up, w_down, out_bias, dy_out):
        n_tok, d_model = x_in.shape
        n_exp = w_router.shape[1]
        top_k = expert_idx.shape[1]
        local_exp = w_gate.shape[0]
        n_ep = n_exp // local_exp
        capacity = (2 * n_tok * top_k + n_exp - 1) // n_exp
        x_f32 = x_in.astype(jnp.float32)
        inv_rms = lax.rsqrt(jnp.mean(x_f32 * x_f32, axis=-1, keepdims=True) + EPS)
        normed = x_f32 * inv_rms
        gain_f32 = norm_gain.astype(jnp.float32)
        hidden = (normed * gain_f32).astype(jnp.bfloat16)
        logits = jnp.dot(hidden, w_router, preferred_element_type=jnp.float32)
        chosen = expert_idx[:, :, None] == jnp.arange(n_exp)[None, None, :]
        gates = jax.nn.softmax(jnp.sum(jnp.where(chosen, logits[:, None, :], 0.0), axis=-1), axis=-1)
        slot_copy, slot_ok, copy_pos = routing_tables(expert_idx, n_exp, capacity)
        place_shape = (n_ep, local_exp, capacity, d_model)
        send_rows = jnp.where(slot_ok[:, :, None], hidden[slot_copy // top_k], 0).reshape(place_shape)
        recv_rows = lax.all_to_all(send_rows, "ep", 0, 0, tiled=True)
        rows_in = lax.all_gather(recv_rows, "tp", axis=0)
        gate_pre = jnp.einsum("tsmcd,mdf->tsmcf", rows_in, w_gate, preferred_element_type=jnp.float32)
        up_pre = jnp.einsum("tsmcd,mdf->tsmcf", rows_in, w_up, preferred_element_type=jnp.float32)
        sigma_gate = jax.nn.sigmoid(gate_pre)
        silu_gate = gate_pre * sigma_gate
        hidden_act = (silu_gate * up_pre).astype(jnp.bfloat16)
        part_out = jnp.einsum("tsmcf,mfd->tsmcd", hidden_act, w_down, preferred_element_type=jnp.float32).astype(jnp.bfloat16)
        y_recv = lax.psum_scatter(part_out, "tp", scatter_dimension=0, tiled=True)[0]
        y_slots = lax.all_to_all(y_recv, "ep", 0, 0, tiled=True).reshape(n_exp * capacity, d_model)
        y_copy = y_slots[copy_pos].astype(jnp.float32)
        moe_out = jnp.sum(gates[:, :, None] * y_copy, axis=1) + out_bias.astype(jnp.float32)
        y_out = (x_f32 + moe_out).astype(jnp.bfloat16)
        dy_f32 = dy_out.astype(jnp.float32)
        d_bias = jnp.sum(dy_f32, axis=0)
        d_gates = jnp.sum(dy_f32[:, None, :] * y_copy, axis=-1)
        dy_copy = (gates[:, :, None] * dy_f32[:, None, :]).astype(jnp.bfloat16).reshape(n_tok * top_k, d_model)
        d_send = jnp.where(slot_ok[:, :, None], dy_copy[slot_copy], 0).reshape(place_shape)
        d_recv = lax.all_to_all(d_send, "ep", 0, 0, tiled=True)
        d_rows = lax.all_gather(d_recv, "tp", axis=0)
        d_act = jnp.einsum("tsmcd,mfd->tsmcf", d_rows, w_down, preferred_element_type=jnp.float32)
        d_down = jnp.einsum("tsmcf,tsmcd->mfd", hidden_act, d_rows, preferred_element_type=jnp.float32)
        d_gate_pre = (d_act * up_pre * sigma_gate * (1.0 + gate_pre * (1.0 - sigma_gate))).astype(jnp.bfloat16)
        d_up_pre = (d_act * silu_gate).astype(jnp.bfloat16)
        d_gate = jnp.einsum("tsmcd,tsmcf->mdf", rows_in, d_gate_pre, preferred_element_type=jnp.float32)
        d_up = jnp.einsum("tsmcd,tsmcf->mdf", rows_in, d_up_pre, preferred_element_type=jnp.float32)
        dh_part = (jnp.einsum("tsmcf,mdf->tsmcd", d_gate_pre, w_gate, preferred_element_type=jnp.float32) + jnp.einsum("tsmcf,mdf->tsmcd", d_up_pre, w_up, preferred_element_type=jnp.float32)).astype(jnp.bfloat16)
        dh_recv = lax.psum_scatter(dh_part, "tp", scatter_dimension=0, tiled=True)[0]
        dh_slots = lax.all_to_all(dh_recv, "ep", 0, 0, tiled=True).reshape(n_exp * capacity, d_model)
        dh_expert = jnp.sum(dh_slots[copy_pos].astype(jnp.float32), axis=1)
        d_chosen = gates * (d_gates - jnp.sum(gates * d_gates, axis=-1, keepdims=True))
        d_logits = jnp.sum(jnp.where(chosen, d_chosen[:, :, None], 0.0), axis=1)
        d_router = jnp.einsum("td,te->de", hidden, d_logits, preferred_element_type=jnp.float32)
        dh_total = dh_expert + jnp.einsum("te,de->td", d_logits, w_router, preferred_element_type=jnp.float32)
        d_gain = jnp.sum(dh_total * normed, axis=0)
        d_norm = dh_total * gain_f32
        dx_in = (dy_f32 + inv_rms * (d_norm - normed * jnp.mean(d_norm * normed, axis=-1, keepdims=True))).astype(jnp.bfloat16)
        d_gain, d_router, d_bias = lax.psum((d_gain, d_router, d_bias), ("ep", "tp"))
        return y_out, dx_in, d_gain, d_router, d_gate, d_up, d_down, d_bias

    return jax.shard_map(device_step, mesh=mesh, in_specs=(tok_spec, P(None), P(None, None), tok_spec, wide_spec, wide_spec, down_spec, P(None), tok_spec), out_specs=(tok_spec, tok_spec, P("dp"), P("dp", None), grad_wide, grad_wide, grad_down, P("dp")), check_vma=False)
```

profile of v0, /device:TPU:0, one launch (start us, length us, event | category | flops | bytes accessed | tf_op | source)
XLA Modules:
  0.0 3215.1 jit_solution(14633073591823256053)
XLA Ops:
  17.0 45.5 %gather_fusion = s32[8192]{0:T(1024)S(1)} fusion(s32[4096]{0:T(1024)S(1)} %get-tuple-element.10, s32[8192]{0:T(1024)S(1)} %broadcast_clamp_fusion.2), kind=kCustom, calls=%fused_computation | custom fusion | bytes 98304 | tf_op jit(solution)/shard_map/gather | solution.py:16
  67.3 35.4 %gather_fusion.1 = bf16[8192,1024]{1,0:T(8,128)(2,1)} fusion(bf16[512,1024]{1,0:T(8,128)(2,1)S(1)} %fusion.51, s32[8192]{0:T(1024)S(1)} %broadcast_clamp_fusion), kind=kCustom, calls=%fused_computation.1 | custom fusion | bytes 33587200 | tf_op jit(solution)/shard_map/gather | solution.py:46
  106.7 45.1 %gather_fusion.3 = bf16[8192,1024]{1,0:T(8,128)(2,1)} fusion(bf16[4096,1024]{1,0:T(8,128)(2,1)} %fusion.13, s32[8192]{0:T(1024)S(1)} %broadcast_clamp_fusion.1), kind=kCustom, calls=%fused_computation.3 | custom fusion | bytes 33587200 | tf_op jit(solution)/shard_map/gather | solution.py:64
  151.8 17.7 broadcast_select_fusion
  169.5 188.3 %all_to_all.20 = bf16[4,8,256,1024]{3,2,1,0:T(8,128)(2,1)} all-to-all(bf16[4,8,256,1024]{3,2,1,0:T(8,128)(2,1)S(1)} %get-tuple-element.56), channel_id=1, replica_groups=mesh['dp'=1,'tp'=2,'ep'=4] {'ep'}, dimensions={0} | all-to-all | bytes 33554432 | tf_op jit(solution)/shard_map/all_to_all | solution.py:47
  357.9 193.8 %all_to_all.21 = bf16[4,8,256,1024]{3,2,1,0:T(8,128)(2,1)} all-to-all(bf16[4,8,256,1024]{3,2,1,0:T(8,128)(2,1)} %get-tuple-element.55), channel_id=1, replica_groups=mesh['dp'=1,'tp'=2,'ep'=4] {'ep'}, dimensions={0} | all-to-all | bytes 33554432 | tf_op jit(solution)/shard_map/all_to_all | solution.py:65
  552.2 192.1 %all-gather.5.cloned.1.call-done = bf16[8,8,256,1024]{3,2,1,0:T(8,128)(2,1)} async-done(((bf16[4,8,256,1024]{3,2,1,0:T(8,128)(2,1)}), bf16[8,8,256,1024]{3,2,1,0:T(8,128)(2,1)}) %all-gather.5.cloned.1.call-update) | async-done | bytes 33554448 | tf_op jit(solution)/shard_map/all_gather | solution.py:48
  744.3 22.6 copy.93
  767.0 19.5 fusion.23
  786.4 19.4 fusion.27
  805.9 325.5 %all-gather.7.cloned.1.call-done = bf16[8,8,256,1024]{3,2,1,0:T(8,128)(2,1)} async-done(((bf16[4,8,256,1024]{3,2,1,0:T(8,128)(2,1)}), bf16[8,8,256,1024]{3,2,1,0:T(8,128)(2,1)}) %all-gather.7.cloned.1.call-update) | async-done | bytes 33554448 | tf_op jit(solution)/shard_map/all_gather | solution.py:66
  1131.4 22.6 copy.97
  1154.0 33.2 %fusion.12 = (bf16[2,4,8,256,256]{4,3,1,0,2:T(8,128)(2,1)}, bf16[2,4,8,256,256]{4,3,1,0,2:T(8,128)(2,1)}, bf16[2,4,8,256,256]{4,3,1,0,2:T(8,128)(2,1)}) fusion(f32[8,2,4,256,256]{4,3,2,1,0:T(8,128)} %fusion.27, f32[8,2,4,256,256]{4,3,2,1,0:T(8,128)} %fusion.23, bf16[2,4,8,256,1024]{4,3,1,0,2:T(8,128)(2,1)} %bitcast.183, bf16[8,256,1024]{2,1,0:T(8,128)(2,1)} %param.15), kind=kOutput, calls=%fused_computation.26 | convolution fusion | flops 8652849152 | bytes 96468992 | tf_op jit(solution)/shard_map/tsmcd,mfd->tsmcf/dot_general | solution.py:67
  1187.3 18.2 convert_bitcast_fusion
  1205.5 27.4 fusion.25
  1232.9 38.1 %fusion = bf16[2,4,8,256,1024]{4,3,1,0,2:T(8,128)(2,1)} fusion(f32[8,2,4,256,1024]{4,3,2,1,0:T(8,128)} %fusion.25, bf16[2,4,8,256,256]{4,3,1,0,2:T(8,128)(2,1)} %get-tuple-element.47, bf16[8,1024,256]{2,1,0:T(8,128)(2,1)} %param.14), kind=kOutput, calls=%fused_computation.6 | convolution fusion | flops 8623489024 | bytes 113246208 | tf_op jit(solution)/shard_map/tsmcf,mdf->tsmcd/dot_general | solution.py:73
  1272.3 1450.4 %all-reduce.9.cloned.1.call-done = (bf16[2,4,8,256,1024]{4,3,1,0,2:T(8,128)(2,1)}, bf16[2,4,8,256,1024]{4,3,1,0,2:T(8,128)(2,1)}) async-done(((bf16[2,4,8,256,1024]{4,3,1,0,2:T(8,128)(2,1)}, bf16[2,4,8,256,1024]{4,3,1,0,2:T(8,128)(2,1)}), (bf16[2,4,8,256,1024]{4,3,1,0,2:T(8,128)(2,1)}, bf16[2,4,8,256,1024]{4,3,1,0,2:T(8,128)(2,1)})) %all-reduce.9.cloned.1.call-update) | async-done | bytes 67108880
  2722.7 8.8 dynamic-slice_bitcast_fusion.1
  2738.1 7.1 all-to-all-start.1
  2745.2 8.8 dynamic-slice_bitcast_fusion
  2760.8 167.1 %all-to-all-done.1 = bf16[4,8,256,1024]{3,2,1,0:T(8,128)(2,1)} async-done(((bf16[4,8,256,1024]{3,2,1,0:T(8,128)(2,1)}), bf16[4,8,256,1024]{3,2,1,0:T(8,128)(2,1)}, u32[]{:S(2)}, u32[]{:S(2)}) %all-to-all-start.1) | async-done | bytes 16777248 | tf_op jit(solution)/shard_map/all_to_all | solution.py:56
  2948.0 15.5 select_subtract_fusion
  2963.8 20.3 fusion.37
  2984.2 19.9 fusion.32
  3004.1 19.9 fusion.42
  3023.9 28.9 gather_fusion.2
  3052.9 10.1 fusion.8
  3063.2 54.5 %all-to-all-done.3 = bf16[4,8,256,1024]{3,2,1,0:T(8,128)(2,1)} async-done(((bf16[4,8,256,1024]{3,2,1,0:T(8,128)(2,1)}), bf16[4,8,256,1024]{3,2,1,0:T(8,128)(2,1)}, u32[]{:S(2)}, u32[]{:S(2)}) %all-to-all-start.3) | async-done | bytes 16777248 | tf_op jit(solution)/shard_map/all_to_all | solution.py:75
  3117.6 28.8 gather_fusion.4
  3146.5 12.1 convert_reduce_fusion
  3167.9 23.3 all-reduce.2
  3191.2 15.6 all-reduce.7.cloned.1.call-done
  (130 shorter events, 64.8 us)
Async XLA Ops:
  7.2 55.9 %copy-start = (bf16[1024,32]{0,1:T(8,128)(2,1)S(1)}, bf16[1024,32]{0,1:T(8,128)(2,1)}, u32[]{:S(2)}) copy-start(bf16[1024,32]{0,1:T(8,128)(2,1)} %param.11) | copy-start | bytes 196612
  7.2 737.1 %all-gather.5.cloned.1.call-start = ((), (), s32[]{:S(2)}) async-start(), calls=%async_computation.5 | async-start | bytes 50331648 | tf_op jit(solution)/shard_map/all_gather | solution.py:48
  8.7 54.0 %copy-start.28 = (f32[512]{0:T(512)}, f32[512]{0:T(512)S(1)}, u32[]{:S(2)}) copy-start(f32[512]{0:T(512)S(1)} %add_rsqrt_fusion) | copy-start | bytes 6148
  9.4 53.3 %copy-start.22 = (f32[1024]{0:T(1024)}, f32[1024]{0:T(1024)S(1)}, u32[]{:S(2)}) copy-start(f32[1024]{0:T(1024)S(1)} %convert_element_type.59) | copy-start | bytes 12292
  10.5 52.1 %copy-start.18 = (s32[4096]{0:T(1024)}, s32[4096]{0:T(1024)S(1)}, u32[]{:S(2)}) copy-start(s32[4096]{0:T(1024)S(1)} %eq.31) | copy-start | bytes 49156
  11.1 51.5 %copy-start.16 = (s32[32]{0:T(128)}, s32[32]{0:T(128)S(1)}, u32[]{:S(2)}) copy-start(s32[32]{0:T(128)S(1)} %sub.53) | copy-start | bytes 388
  16.9 45.7 %copy-start.1 = (s32[4096]{0:T(1024)}, s32[4096]{0:T(1024)S(1)}, u32[]{:S(2)}) copy-start(s32[4096]{0:T(1024)S(1)} %get-tuple-element.10) | copy-start | bytes 49156
  17.0 45.8 %copy-start.7 = (bf16[512,1024]{1,0:T(8,128)(2,1)S(1)}, bf16[512,1024]{1,0:T(8,128)(2,1)}, u32[]{:S(2)}) copy-start(bf16[512,1024]{1,0:T(8,128)(2,1)} %param.9) | copy-start | bytes 3145732
  17.0 46.5 %copy-start.20 = (s32[512,8]{0,1:T(8,128)S(1)}, s32[512,8]{0,1:T(8,128)}, u32[]{:S(2)}) copy-start(s32[512,8]{0,1:T(8,128)} %param.12) | copy-start | bytes 49156
  63.1 39.6 %copy-start.3 = (bf16[512,1024]{1,0:T(8,128)(2,1)}, bf16[512,1024]{1,0:T(8,128)(2,1)S(1)}, u32[]{:S(2)}) copy-start(bf16[512,1024]{1,0:T(8,128)(2,1)S(1)} %fusion.51) | copy-start | bytes 3145732
  67.3 35.5 %copy-start.5 = (f32[512,1024]{1,0:T(8,128)}, f32[512,1024]{1,0:T(8,128)S(1)}, u32[]{:S(2)}) copy-start(f32[512,1024]{1,0:T(8,128)S(1)} %convert_element_type.68) | copy-start | bytes 6291460
  357.8 773.5 %all-gather.7.cloned.1.call-start = ((), (), s32[]{:S(2)}) async-start(), calls=%async_computation.6 | async-start | bytes 50331648 | tf_op jit(solution)/shard_map/all_gather | solution.py:66
  551.7 2171.0 %all-reduce.9.cloned.1.call-start = ((), (), s32[]{:S(2)}) async-start(), calls=%async_computation.7 | async-start | bytes 134217728
  2738.1 189.8 %all-to-all-start.1 = ((bf16[4,8,256,1024]{3,2,1,0:T(8,128)(2,1)}), bf16[4,8,256,1024]{3,2,1,0:T(8,128)(2,1)}, u32[]{:S(2)}, u32[]{:S(2)}) async-start(bf16[4,8,256,1024]{3,2,1,0:T(8,128)(2,1)} %copy.94), calls=%async_computation.1 | async-start | bytes 33554432 | tf_op jit(solution)/shard_map/all_to_all | solution.py:56
  2760.8 174.2 %copy-start.13 = (s32[512,8]{1,0:T(8,128)S(1)}, s32[512,8]{1,0:T(8,128)}, u32[]{:S(2)}) copy-start(s32[512,8]{1,0:T(8,128)} %copy-done.12) | copy-start | bytes 49156
  2760.8 174.4 %copy-start.30 = (bf16[1024]{0:T(1024)(128)(2,1)S(1)}, bf16[1024]{0:T(1024)(128)(2,1)}, u32[]{:S(2)}) copy-start(bf16[1024]{0:T(1024)(128)(2,1)} %param.16) | copy-start | bytes 6148
  2760.8 174.4 %copy-start.2 = (s32[4096]{0:T(1024)S(1)}, s32[4096]{0:T(1024)}, u32[]{:S(2)}) copy-start(s32[4096]{0:T(1024)} %copy-done.1) | copy-start | bytes 49156
  2760.8 180.2 %copy-start.17 = (s32[32]{0:T(128)S(1)}, s32[32]{0:T(128)}, u32[]{:S(2)}) copy-start(s32[32]{0:T(128)} %copy-done.16) | copy-start | bytes 388
  2760.8 187.2 %copy-start.19 = (s32[4096]{0:T(1024)S(1)}, s32[4096]{0:T(1024)}, u32[]{:S(2)}) copy-start(s32[4096]{0:T(1024)} %copy-done.18) | copy-start | bytes 49156
  2927.9 189.7 %all-to-all-start.3 = ((bf16[4,8,256,1024]{3,2,1,0:T(8,128)(2,1)}), bf16[4,8,256,1024]{3,2,1,0:T(8,128)(2,1)}, u32[]{:S(2)}, u32[]{:S(2)}) async-start(bf16[4,8,256,1024]{3,2,1,0:T(8,128)(2,1)} %copy.98), calls=%async_computation.3 | async-start | bytes 33554432 | tf_op jit(solution)/shard_map/all_to_all | solution.py:75
  2934.9 271.9 %all-reduce.7.cloned.1.call-start = ((), (), s32[]{:S(2)}) async-start(), calls=%async_computation.4 | async-start | bytes 262144 | tf_op jit(solution)/shard_map/psum | solution.py:84
  3023.9 28.9 copy-start.6
  3023.9 28.9 copy-start.11
  3052.8 10.2 copy-start.15
  3052.8 10.2 copy-start.25
  3052.8 10.2 copy-start.27
  3146.4 12.1 copy-start.21
  3146.4 12.2 copy-start.4
  3146.4 13.2 copy-start.8
  3146.4 13.2 copy-start.23
  3146.4 13.1 copy-start.29
  3146.5 16.9 copy-start.9
  (6 other events, 3.9 us)
Sparse Core Ops, SparseCore 0:
  358.0 386.3 all-gather.4
  745.8 385.4 all-gather.6
  1271.2 1451.4 all-reduce.8
  3163.4 43.3 all-reduce.6
where the time goes:
time: 3220 us
  waiting for transfers between devices  2210 us (69%)
  blocking collectives  405 us (13%)
  local copies, waits for them, and re-layouts  268 us (8%)
  matrix products  221 us (7%)
  other arithmetic  85.9 us (3%)
    unnamed x5, waiting for transfers between devices  1450 us
    all_gather x1, waiting for transfers between devices, device_step(): d_rows = lax.all_gather(d_recv, 'tp', axis=0)  326 us
    all_to_all x1, blocking collectives, device_step(): d_recv = lax.all_to_all(d_send, 'ep', 0, 0, tiled=True)  194 us
    all_gather x1, waiting for transfers between devices, device_step(): rows_in = lax.all_gather(recv_rows, 'tp', axis=0)  192 us
    all_to_all x1, blocking collectives, device_step(): recv_rows = lax.all_to_all(send_rows, 'ep', 0, 0, tiled=True)  188 us
    all_to_all x1, waiting for transfers between devices, device_step(): lax.all_to_all(y_recv, 'ep', 0, 0, tiled=True)  167 us
  transfers between devices with their start and end apart: 6, of which 6 were waited for; matrix products, arithmetic and copies ran while one was open for 7% of the time, Pallas kernels for 0%

commit v1 on v0

v1 whole, which is shorter than its diff:
```python
import functools

import jax
import jax.numpy as jnp
from jax import lax
from jax.experimental import pallas as pl
from jax.experimental.pallas import tpu as pltpu
from jax.sharding import PartitionSpec as P

EPS = 1e-6
F32 = jnp.float32
BF16 = jnp.bfloat16


def dot_nn(a, b):
    return jnp.dot(a, b, preferred_element_type=F32)


def dot_nt(a, b):
    return lax.dot_general(a, b, (((1,), (1,)), ((), ())), preferred_element_type=F32)


def dot_tn(a, b):
    return lax.dot_general(a, b, (((0,), (0,)), ((), ())), preferred_element_type=F32)


def expert_step(e, first, h_ref, ht_ref, dy_ref, g_ref, wgu, wd, dwgu, dwd, out_acc, dh_acc, dg_acc):
    half = wd.shape[1]
    rows = h_ref.shape[0]
    lane = lax.broadcasted_iota(jnp.int32, (rows, 128), 1)
    gate = jnp.sum(jnp.where(lane == e, g_ref[...], 0.0), axis=1, keepdims=True)
    on = gate > 0.0
    au = dot_nn(h_ref[...], wgu[e])
    raw = dot_nt(dy_ref[...], wd[e])
    a = au[:, :half]
    u = au[:, half:]
    sig = jax.nn.sigmoid(a)
    silu = a * sig
    act = jnp.where(on, silu * u, 0.0).astype(BF16)
    dg = jnp.sum(jnp.where(on, act.astype(F32) * raw, 0.0), axis=1, keepdims=True)
    dg_acc[...] = jnp.where(lane == e, dg, dg_acc[...])
    d_act = gate * raw
    da = jnp.where(on, d_act * u * sig * (1.0 + a * (1.0 - sig)), 0.0).astype(BF16)
    du = jnp.where(on, d_act * silu, 0.0).astype(BF16)
    dau = jnp.concatenate([da, du], axis=1)
    out_acc[...] += gate * dot_nn(act, wd[e])
    dh_acc[...] += dot_nt(dau, wgu[e])
    dwgu[e] += dot_nn(ht_ref[...], dau)
    gdy = (gate * dy_ref[...].astype(F32)).astype(BF16)
    dwd[e] += dot_tn(act, gdy)


def dense_kernel(h_hbm, dy_hbm, g_hbm, wg_hbm, wu_hbm, wd_hbm, tok_hbm, dg_hbm, dwg_hbm, dwu_hbm, dwd_hbm,
                 h_s, dy_s, g_s, ht_s, wgu, wd, dwgu, dwd, out_acc, dh_acc, dg_acc, tok_s, dg_s,
                 in_sem, w_sem, out_sem, dw_sem):
    n_blk, rows, d = h_hbm.shape
    n_loc, _, half = wg_hbm.shape

    def loads(c, slot):
        return [pltpu.make_async_copy(h_hbm.at[c], h_s.at[slot], in_sem.at[slot, 0]),
                pltpu.make_async_copy(dy_hbm.at[c], dy_s.at[slot], in_sem.at[slot, 1]),
                pltpu.make_async_copy(g_hbm.at[c], g_s.at[slot], in_sem.at[slot, 2])]

    def w_loads(e):
        return [pltpu.make_async_copy(wg_hbm.at[e], wgu.at[e, :, pl.ds(0, half)], w_sem.at[e, 0]),
                pltpu.make_async_copy(wu_hbm.at[e], wgu.at[e, :, pl.ds(half, half)], w_sem.at[e, 1]),
                pltpu.make_async_copy(wd_hbm.at[e], wd.at[e], w_sem.at[e, 2])]

    def dw_stores(e):
        return [pltpu.make_async_copy(dwgu.at[e, :, pl.ds(0, half)], dwg_hbm.at[e], dw_sem.at[e, 0]),
                pltpu.make_async_copy(dwgu.at[e, :, pl.ds(half, half)], dwu_hbm.at[e], dw_sem.at[e, 1]),
                pltpu.make_async_copy(dwd.at[e], dwd_hbm.at[e], dw_sem.at[e, 2])]

    def out_stores(c):
        return [pltpu.make_async_copy(tok_s, tok_hbm.at[c], out_sem.at[0]),
                pltpu.make_async_copy(dg_s, dg_hbm.at[c], out_sem.at[1])]

    for cp in loads(0, 0):
        cp.start()

    def start_w(e, _):
        for cp in w_loads(e):
            cp.start()
        return 0
    lax.fori_loop(0, n_loc, start_w, 0)

    def block(c, _):
        slot = lax.rem(c, 2)
        for cp in loads(c, slot):
            cp.wait()

        @pl.when(c + 1 < n_blk)
        def _():
            for cp in loads(c + 1, 1 - slot):
                cp.start()
        h_ref, dy_ref, g_ref = h_s.at[slot], dy_s.at[slot], g_s.at[slot]
        ht_s[...] = h_ref[...].T
        out_acc[...] = jnp.zeros_like(out_acc)
        dh_acc[...] = jnp.zeros_like(dh_acc)
        dg_acc[...] = jnp.zeros_like(dg_acc)

        def expert(e, _):
            @pl.when(c == 0)
            def _():
                for cp in w_loads(e):
                    cp.wait()
                dwgu[e] = jnp.zeros(dwgu.shape[1:], F32)
                dwd[e] = jnp.zeros(dwd.shape[1:], F32)
            expert_step(e, None, h_ref, ht_s, dy_ref, g_ref, wgu, wd, dwgu, dwd, out_acc, dh_acc, dg_acc)

            @pl.when(c == n_blk - 1)
            def _():
                for cp in dw_stores(e):
                    cp.start()
            return 0
        lax.fori_loop(0, n_loc, expert, 0)

        @pl.when(c > 0)
        def _():
            for cp in out_stores(c - 1):
                cp.wait()
        tok_s[:, pl.ds(0, d)] = out_acc[...].astype(BF16)
        tok_s[:, pl.ds(d, d)] = dh_acc[...].astype(BF16)
        dg_s[...] = dg_acc[...]
        for cp in out_stores(c):
            cp.start()
        return 0
    lax.fori_loop(0, n_blk, block, 0)
    for cp in out_stores(n_blk - 1):
        cp.wait()

    def end_w(e, _):
        for cp in dw_stores(e):
            cp.wait()
        return 0
    lax.fori_loop(0, n_loc, end_w, 0)


def dense_experts(h_all, dy_all, g_all, w_gate, w_up, w_down):
    n_blk, rows, d = h_all.shape
    n_loc, _, half = w_gate.shape
    flops = 18 * n_blk * rows * n_loc * d * half
    return pl.pallas_call(
        dense_kernel,
        out_shape=[jax.ShapeDtypeStruct((n_blk, rows, 2 * d), BF16),
                   jax.ShapeDtypeStruct((n_blk, rows, 128), F32),
                   jax.ShapeDtypeStruct(w_gate.shape, F32),
                   jax.ShapeDtypeStruct(w_up.shape, F32),
                   jax.ShapeDtypeStruct(w_down.shape, F32)],
        in_specs=[pl.BlockSpec(memory_space=pl.ANY)] * 6,
        out_specs=[pl.BlockSpec(memory_space=pl.ANY)] * 5,
        scratch_shapes=[
            pltpu.VMEM((2, rows, d), BF16), pltpu.VMEM((2, rows, d), BF16), pltpu.VMEM((2, rows, 128), F32),
            pltpu.VMEM((d, rows), BF16),
            pltpu.VMEM((n_loc, d, 2 * half), BF16), pltpu.VMEM((n_loc, half, d), BF16),
            pltpu.VMEM((n_loc, d, 2 * half), F32), pltpu.VMEM((n_loc, half, d), F32),
            pltpu.VMEM((rows, d), F32), pltpu.VMEM((rows, d), F32), pltpu.VMEM((rows, 128), F32),
            pltpu.VMEM((rows, 2 * d), BF16), pltpu.VMEM((rows, 128), F32),
            pltpu.SemaphoreType.DMA((2, 3)), pltpu.SemaphoreType.DMA((n_loc, 3)),
            pltpu.SemaphoreType.DMA((2,)), pltpu.SemaphoreType.DMA((n_loc, 3)),
        ],
        compiler_params=pltpu.CompilerParams(vmem_limit_bytes=66_000_000),
        cost_estimate=pl.CostEstimate(flops=flops, bytes_accessed=100_000_000, transcendentals=0),
        name="dense_experts",
    )(h_all, dy_all, g_all, w_gate, w_up, w_down)


def solution(mesh):
    tok_spec = P(("dp", "ep", "tp"), None)
    wide_spec = P("ep", None, "tp")
    down_spec = P("ep", "tp", None)
    grad_wide = P(("dp", "ep"), None, "tp")
    grad_down = P(("dp", "ep"), "tp", None)

    def device_step(x_in, norm_gain, w_router, expert_idx, w_gate, w_up, w_down, out_bias, dy_out):
        n_tok, d = x_in.shape
        n_exp = w_router.shape[1]
        n_loc = w_gate.shape[0]
        group = ("ep", "tp")
        x_f32 = x_in.astype(F32)
        inv_rms = lax.rsqrt(jnp.mean(x_f32 * x_f32, axis=-1, keepdims=True) + EPS)
        normed = x_f32 * inv_rms
        gain = norm_gain.astype(F32)
        hidden = (normed * gain).astype(BF16)
        logits = jnp.dot(hidden, w_router, preferred_element_type=F32)
        chosen = jnp.any(expert_idx[:, :, None] == jnp.arange(n_exp)[None, None, :], axis=1)
        gates = jax.nn.softmax(jnp.where(chosen, logits, -jnp.inf), axis=-1)
        h_all = lax.all_gather(hidden, group, axis=0)
        dy_all = lax.all_gather(dy_out, group, axis=0)
        g_all = lax.all_gather(gates, group, axis=0)
        my_ep = lax.axis_index("ep")
        g_loc = lax.dynamic_slice_in_dim(g_all, my_ep * n_loc, n_loc, axis=2)
        g_loc = jnp.pad(g_loc, ((0, 0), (0, 0), (0, 128 - n_loc)))
        tok, dg, d_gate, d_up, d_down = dense_experts(h_all, dy_all, g_loc, w_gate, w_up, w_down)
        tok = lax.psum_scatter(tok.reshape(-1, 2 * d), group, scatter_dimension=0, tiled=True)
        dg = lax.all_to_all(dg[:, :, :n_loc], group, 0, 0, tiled=True)
        dg = jnp.sum(dg.reshape(n_exp // n_loc, -1, n_tok, n_loc), axis=1)
        d_gates = jnp.transpose(dg, (1, 0, 2)).reshape(n_tok, n_exp)
        moe_out = tok[:, :d].astype(F32) + out_bias.astype(F32)
        y_out = (x_f32 + moe_out).astype(BF16)
        dy_f32 = dy_out.astype(F32)
        d_bias = jnp.sum(dy_f32, axis=0)
        d_logits = gates * (d_gates - jnp.sum(gates * d_gates, axis=-1, keepdims=True))
        d_router = jnp.einsum("td,te->de", hidden, d_logits, preferred_element_type=F32)
        dh_total = tok[:, d:].astype(F32) + jnp.einsum("te,de->td", d_logits, w_router, preferred_element_type=F32)
        d_gain = jnp.sum(dh_total * normed, axis=0)
        d_norm = dh_total * gain
        dx_in = (dy_f32 + inv_rms * (d_norm - normed * jnp.mean(d_norm * normed, axis=-1, keepdims=True))).astype(BF16)
        d_gain, d_router, d_bias = lax.psum((d_gain, d_router, d_bias), group)
        return y_out, dx_in, d_gain, d_router, d_gate, d_up, d_down, d_bias

    return jax.shard_map(device_step, mesh=mesh, in_specs=(tok_spec, P(None), P(None, None), tok_spec, wide_spec, wide_spec, down_spec, P(None), tok_spec), out_specs=(tok_spec, tok_spec, P("dp"), P("dp", None), grad_wide, grad_wide, grad_down, P("dp")), check_vma=False)
```

time: 3220 us -> 473 us (0.15)
  waiting for transfers between devices: 2210 us -> 200 us
  blocking collectives: 405 us -> 41.1 us
  local copies, waits for them, and re-layouts: 268 us -> 9.44 us
  matrix products: 221 us -> 3.62 us
  Pallas kernels: 0 us -> 196 us
  other arithmetic: 85.9 us -> 7.27 us
    unnamed x5 -> x4, waiting for transfers between devices: 1450 us -> 0.75 us
    all_gather x2, waiting for transfers between devices: 518 us -> 79.5 us  [the longest x1 50.2 us: device_step(): dy_all = lax.all_gather(dy_out, group, axis=0)]
    all_to_all x2 -> x0, blocking collectives: 382 us -> none  [the longest x1 194 us: device_step(): d_recv = lax.all_to_all(d_send, 'ep', 0, 0, tiled=True)]
    dot_general x12 -> x3, matrix products: 221 us -> 3.62 us  [the longest x1 2.25 us: device_step(): jnp.einsum('te,de->td', d_logits, w_router, preferred_element_type=F32)]
    all_to_all x2 -> x1, waiting for transfers between devices: 222 us -> 4.63 us  [device_step(): dg = lax.all_to_all(dg[:, :, :n_loc], group, 0, 0, tiled=True)]
    pallas_call x0 -> x1, Pallas kernels: none -> 196 us  [dense_experts(): pl.pallas_call(dense_kernel, out_shape=[jax.ShapeDtypeStruct((n_blk, rows...]
    gather x8 -> x0, local copies, waits for them, and re-layouts: 185 us -> none  [the longest x2 45.5 us: routing_tables(): order[jnp.minimum(starts[:, None] + slot_rank, n_tok * top_k - 1)]]
    reduce_scatter x0 -> x1, waiting for transfers between devices: none -> 96.1 us  [device_step(): lax.psum_scatter(tok.reshape(-1, 2 * d), group, scatter_dimension=0, tile...]
  transfers between devices with their start and end apart: 6 -> 5, of which waited for: 6 -> 5; matrix products, arithmetic and copies ran while one was open for 7% -> 3% of each run, Pallas kernels for 0% -> 0%
where the time goes in v1:
time: 473 us
  waiting for transfers between devices  200 us (42%)
  Pallas kernels  196 us (41%)
  blocking collectives  41.1 us (9%)
  between operations  14 us (3%)
  local copies, waits for them, and re-layouts  9.44 us (2%)
  other arithmetic  7.27 us (2%)
    pallas_call x1, Pallas kernels, dense_experts(): pl.pallas_call(dense_kernel, out_shape=[jax.ShapeDtypeStruct((n_blk, rows...  196 us
    reduce_scatter x1, waiting for transfers between devices, device_step(): lax.psum_scatter(tok.reshape(-1, 2 * d), group, scatter_dimension=0, tile...  96.1 us
    all_gather x1, waiting for transfers between devices, device_step(): dy_all = lax.all_gather(dy_out, group, axis=0)  50.2 us
    all_gather x1, waiting for transfers between devices, device_step(): h_all = lax.all_gather(hidden, group, axis=0)  29.3 us
    psum x1, blocking collectives, device_step(): d_gain, d_router, d_bias = lax.psum((d_gain, d_router, d_bias), group)  22.3 us
    all_gather x1, blocking collectives, device_step(): g_all = lax.all_gather(gates, group, axis=0)  18.8 us
    psum x1, waiting for transfers between devices, device_step(): d_gain, d_router, d_bias = lax.psum((d_gain, d_router, d_bias), group)  18.7 us
  transfers between devices with their start and end apart: 5, of which 5 were waited for; matrix products, arithmetic and copies ran while one was open for 3% of the time, Pallas kernels for 0%

profile of v1, /device:TPU:0, one launch (start us, length us, event | category | flops | bytes accessed | tf_op | source)
XLA Modules:
  0.0 473.0 jit_solution(6123400832954494797)
XLA Ops:
  7.2 0.0 all-gather.6.cloned.1.call-start
  7.2 1.5 fusion.10
  8.8 0.7 convert_element_type.30
  9.4 0.6 copy-done.10
  10.0 2.5 fusion.5
  12.6 0.0 all-gather.8.cloned.1.call-start
  12.6 0.7 all-gather.8.cloned.1.call-update
  13.3 0.0 reduce-scatter.2.cloned.1.call-start
  13.4 0.1 fusion.12
  13.5 0.3 copy-done.1
  13.8 0.4 fusion.20
  14.3 0.5 copy-done.5
  14.8 0.0 copy-done.12
  14.9 0.6 copy-done.7
  15.5 18.8 %all-gather.2 = f32[4096,32]{0,1:T(8,128)S(1)} all-gather(f32[512,32]{0,1:T(8,128)S(1)} %fusion.15), channel_id=4, replica_groups=mesh['dp'=1,'tp'=2,'ep'=4] {'ep','tp'}, dimensions={0}, use_global_device_ids=true | all-gather | bytes 589824 | tf_op jit(solution)/shard_map/all_gather | solution.py:190
  34.3 0.6 copy.24
  34.9 0.6 constant_dynamic-slice_fusion
  35.5 1.5 pad.4.g_hbm
  37.0 29.3 %all-gather.6.cloned.1.call-done = bf16[4096,1024]{1,0:T(8,128)(2,1)} async-done(((bf16[512,1024]{1,0:T(8,128)(2,1)}), bf16[4096,1024]{1,0:T(8,128)(2,1)}) %all-gather.6.cloned.1.call-update) | async-done | bytes 8388624 | tf_op jit(solution)/shard_map/all_gather | solution.py:188
  66.4 50.2 %all-gather.8.cloned.1.call-done = bf16[4096,1024]{1,0:T(8,128)(2,1)} async-done(((bf16[512,1024]{1,0:T(8,128)(2,1)}), bf16[4096,1024]{1,0:T(8,128)(2,1)}) %all-gather.8.cloned.1.call-update) | async-done | bytes 8388624 | tf_op jit(solution)/shard_map/all_gather | solution.py:189
  116.5 195.6 %dense_experts.1 = (bf16[8,512,2048]{2,1,0:T(8,128)(2,1)}, f32[8,512,128]{2,1,0:T(8,128)}, f32[8,1024,256]{2,1,0:T(8,128)}, f32[8,1024,256]{2,1,0:T(8,128)}, f32[8,256,1024]{2,1,0:T(8,128)}) custom-call(bf16[8,512,1024]{2,1,0:T(8,128)(2,1)} %bitcast.28, bf16[8,512,1024]{2,1,0:T(8,128)(2,1)} %bitcast.29, f32[8,512,128]{2,1,0:T(8,128)} %pad.4.g_hbm, ...), custom_call_target="tpu_custom_call" | custom-call | flops 154618822656 | bytes 100000000 | tf_op jit(solution)/shard_map/dense_experts/pallas_call | solution.py:143
  312.3 3.0 copy.25
  315.3 2.1 all-to-all-start
  317.4 0.0 all-reduce.4.cloned.1.call-start
  317.4 4.6 all-to-all-done
  322.2 0.9 fusion.17
  323.2 96.1 %reduce-scatter.2.cloned.1.call-done = bf16[512,2048]{1,0:T(8,128)(2,1)} async-done(((bf16[4096,2048]{1,0:T(8,128)(2,1)}), bf16[512,2048]{1,0:T(8,128)(2,1)}) %reduce-scatter.2.cloned.1.call-update) | async-done | bytes 2097168 | tf_op jit(solution)/shard_map/reduce_scatter | solution.py:195
  419.3 2.3 fusion.9
  421.6 2.4 convert_reduce_fusion
  424.0 22.3 %all-reduce.1 = (f32[1024]{0:T(1024)}, f32[1024]{0:T(1024)}) all-reduce(f32[1024]{0:T(1024)S(1)} %get-tuple-element.18, f32[1024]{0:T(1024)S(1)} %get-tuple-element.22), channel_id=1, replica_groups=mesh['dp'=1,'tp'=2,'ep'=4] {'ep','tp'}, use_global_device_ids=true, to_apply=%region_9.10 | all-reduce | flops 2048 | bytes 16384 | tf_op jit(solution)/shard_map/psum | solution.py:209
  446.2 18.7 %all-reduce.4.cloned.1.call-done = f32[1024,32]{0,1:T(8,128)} async-done(((f32[1024,32]{0,1:T(8,128)}), f32[1024,32]{0,1:T(8,128)}) %all-reduce.4.cloned.1.call-update) | async-done | bytes 131088 | tf_op jit(solution)/shard_map/psum | solution.py:209
  464.9 1.6 copy.31
  (45 shorter events, 0.3 us)
Async XLA Ops:
  7.2 6.3 %copy-start = (bf16[1024,32]{0,1:T(8,128)(2,1)S(1)}, bf16[1024,32]{0,1:T(8,128)(2,1)}, u32[]{:S(2)}) copy-start(bf16[1024,32]{0,1:T(8,128)(2,1)} %param.11) | copy-start | bytes 196612
  7.2 59.2 %all-gather.6.cloned.1.call-start = ((), (), s32[]{:S(2)}) async-start(), calls=%async_computation.4 | async-start | bytes 9437184 | tf_op jit(solution)/shard_map/all_gather | solution.py:188
  8.7 0.7 copy-start.16
  9.4 0.6 copy-start.10
  10.0 3.3 copy-start.18
  12.6 1.2 copy-start.1
  12.6 104.0 %all-gather.8.cloned.1.call-start = ((), (), s32[]{:S(2)}) async-start(), calls=%async_computation.5 | async-start | bytes 9437184 | tf_op jit(solution)/shard_map/all_gather | solution.py:189
  13.3 406.0 %reduce-scatter.2.cloned.1.call-start = ((), (), s32[]{:S(2)}) async-start(), calls=%async_computation.2 | async-start | bytes 18874368 | tf_op jit(solution)/shard_map/reduce_scatter | solution.py:195
  14.2 0.6 copy-start.5
  14.2 0.6 copy-start.12
  14.3 0.6 copy-start.14
  14.9 0.6 copy-start.7
  312.2 5.2 %copy-start.19 = (bf16[1024]{0:T(1024)(128)(2,1)S(1)}, bf16[1024]{0:T(1024)(128)(2,1)}, u32[]{:S(2)}) copy-start(bf16[1024]{0:T(1024)(128)(2,1)} %param.16) | copy-start | bytes 6148
  312.2 9.9 %copy-start.6 = (f32[512,32]{0,1:T(8,128)S(1)}, f32[512,32]{0,1:T(8,128)}, u32[]{:S(2)}) copy-start(f32[512,32]{0,1:T(8,128)} %copy-done.5) | copy-start | bytes 196612
  312.2 9.9 %copy-start.13 = (f32[512]{0:T(512)S(1)}, f32[512]{0:T(512)}, u32[]{:S(2)}) copy-start(f32[512]{0:T(512)} %copy-done.12) | copy-start | bytes 6148
  312.2 9.9 %copy-start.15 = (f32[512]{0:T(512)S(1)}, f32[512]{0:T(512)}, u32[]{:S(2)}) copy-start(f32[512]{0:T(512)} %copy-done.14) | copy-start | bytes 6148
  312.2 9.9 %copy-start.2 = (bf16[512,1024]{1,0:T(8,128)(2,1)S(1)}, bf16[512,1024]{1,0:T(8,128)(2,1)}, u32[]{:S(2)}) copy-start(bf16[512,1024]{1,0:T(8,128)(2,1)} %fusion.5) | copy-start | bytes 3145732
  312.2 9.9 %copy-start.8 = (f32[512,32]{0,1:T(8,128)S(1)}, f32[512,32]{0,1:T(8,128)}, u32[]{:S(2)}) copy-start(f32[512,32]{0,1:T(8,128)} %copy-done.7) | copy-start | bytes 196612
  312.3 107.0 %copy-start.3 = (bf16[512,1024]{1,0:T(8,128)(2,1)S(1)}, bf16[512,1024]{1,0:T(8,128)(2,1)}, u32[]{:S(2)}) copy-start(bf16[512,1024]{1,0:T(8,128)(2,1)} %param.9) | copy-start | bytes 3145732
  312.3 107.0 %copy-start.11 = (f32[1024]{0:T(1024)S(1)}, f32[1024]{0:T(1024)}, u32[]{:S(2)}) copy-start(f32[1024]{0:T(1024)} %copy-done.10) | copy-start | bytes 12292
  312.3 107.0 %copy-start.17 = (f32[512]{0:T(512)S(1)}, f32[512]{0:T(512)}, u32[]{:S(2)}) copy-start(f32[512]{0:T(512)} %copy-done.16) | copy-start | bytes 6148
  315.3 6.8 %all-to-all-start = ((f32[8,512,8]{1,2,0:T(8,128)}), f32[8,512,8]{1,2,0:T(8,128)S(1)}, u32[]{:S(2)}, u32[]{:S(2)}) async-start(f32[8,512,8]{1,2,0:T(8,128)} %copy.25), calls=%async_computation.1 | async-start | bytes 262144 | tf_op jit(solution)/shard_map/all_to_all | solution.py:196
  317.4 147.6 %all-reduce.4.cloned.1.call-start = ((), (), s32[]{:S(2)}) async-start(), calls=%async_computation.3 | async-start | bytes 262144 | tf_op jit(solution)/shard_map/psum | solution.py:209
  323.1 98.4 %copy-start.4 = (bf16[512,1024]{1,0:T(8,128)(2,1)S(1)}, bf16[512,1024]{1,0:T(8,128)(2,1)}, u32[]{:S(2)}) copy-start(bf16[512,1024]{1,0:T(8,128)(2,1)} %param.17) | copy-start | bytes 3145732
  419.3 2.3 copy-start.9
Sparse Core Ops, SparseCore 0:
  12.7 53.6 all-gather.5
  68.2 48.3 all-gather.7
  312.3 106.9 reduce-scatter.1
  422.7 42.1 all-reduce.3

commit v2 on v1

v2 whole, which is shorter than its diff:
```python
import functools

import jax
import jax.numpy as jnp
from jax import lax
from jax.experimental import pallas as pl
from jax.experimental.pallas import tpu as pltpu
from jax.sharding import PartitionSpec as P

EPS = 1e-6
F32 = jnp.float32
BF16 = jnp.bfloat16


def dot_nn(a, b):
    return jnp.dot(a, b, preferred_element_type=F32)


def dot_nt(a, b):
    return lax.dot_general(a, b, (((1,), (1,)), ((), ())), preferred_element_type=F32)


def dot_tn(a, b):
    return lax.dot_general(a, b, (((0,), (0,)), ((), ())), preferred_element_type=F32)


def expert_step(e, first, h_ref, ht_ref, dy_ref, g_ref, wgu, wd, dwgu, dwd, out_acc, dh_acc, dg_acc):
    half = wd.shape[1]
    rows = h_ref.shape[0]
    lane = lax.broadcasted_iota(jnp.int32, (rows, 128), 1)
    gate = jnp.sum(jnp.where(lane == e, g_ref[...], 0.0), axis=1, keepdims=True)
    on = gate > 0.0
    au = dot_nn(h_ref[...], wgu[e])
    raw = dot_nt(dy_ref[...], wd[e])
    a = au[:, :half]
    u = au[:, half:]
    sig = jax.nn.sigmoid(a)
    silu = a * sig
    act = jnp.where(on, silu * u, 0.0).astype(BF16)
    dg = jnp.sum(jnp.where(on, act.astype(F32) * raw, 0.0), axis=1, keepdims=True)
    dg_acc[...] = jnp.where(lane == e, dg, dg_acc[...])
    d_act = gate * raw
    da = jnp.where(on, d_act * u * sig * (1.0 + a * (1.0 - sig)), 0.0).astype(BF16)
    du = jnp.where(on, d_act * silu, 0.0).astype(BF16)
    dau = jnp.concatenate([da, du], axis=1)
    out_acc[...] += gate * dot_nn(act, wd[e])
    dh_acc[...] += dot_nt(dau, wgu[e])
    dwgu[e] += dot_nn(ht_ref[...], dau)
    gdy = (gate * dy_ref[...].astype(F32)).astype(BF16)
    dwd[e] += dot_tn(act, gdy)


FLIPS = ((0, 0, 0), (0, 0, 1), (1, 0, 1), (0, 1, 0), (1, 1, 1), (1, 1, 0), (0, 1, 1), (1, 0, 0))
MIRROR = (0, 1, 6, 3, 4, 5, 2, 7)


def place(step):
    fa, fb, fc = FLIPS[step]
    ep = lax.axis_index("ep")
    y = lax.axis_index("tp")
    x = ep // 2
    c = ep % 2
    fx = fa * (1 - c) + fb * c
    fy = fa * c + fb * (1 - c)
    x2 = x + fx * (1 - 2 * x)
    y2 = y + fy * (1 - 2 * y)
    c2 = c + fc * (1 - 2 * c)
    return 2 * x2 + c2, y2


def dense_kernel(h_hbm, dy_hbm, gt_hbm, wg_hbm, wu_hbm, wd_hbm,
                 tok_own, tok_recv, dg_recv, h_buf, dy_buf, g_buf, dwg_hbm, dwu_hbm, dwd_hbm,
                 h_s, dy_s, gt_s, g_s, ht_s, wgu, wd, dwgu, dwd, out_acc, dh_acc, dg_acc, tok_s, dgt_s, pair_s,
                 in_sem, w_sem, dw_sem, ag_send, ag_recv, g_send, g_recv, tok_send, tok_rsem, pair_rsem, dg_send, dg_rsem, own_sem):
    rows, d = h_hbm.shape
    n_loc, _, half = wg_hbm.shape
    n_blk = len(FLIPS)
    my_ep = lax.axis_index("ep")
    my_blk = 2 * my_ep + lax.axis_index("tp")

    def remote(src, dst, send, recv, step):
        ep, tp = place(step)
        return pltpu.make_async_remote_copy(src_ref=src, dst_ref=dst, send_sem=send, recv_sem=recv,
                                            device_id={"ep": ep, "tp": tp}, device_id_type=pl.DeviceIdType.MESH)

    def rows_copy(i, src_step, dst_step, slot):
        hs = h_hbm if src_step == 0 else h_buf.at[src_step]
        ds = dy_hbm if src_step == 0 else dy_buf.at[src_step]
        return [remote(hs, h_buf.at[slot], ag_send.at[i, 0], ag_recv.at[slot, 0], dst_step),
                remote(ds, dy_buf.at[slot], ag_send.at[i, 1], ag_recv.at[slot, 1], dst_step)]

    own_to_partner = rows_copy(0, 0, 1, 1)
    own_to_b = rows_copy(1, 0, 3, 3)
    b_to_partner = rows_copy(2, 3, 1, 2)
    b_to_a = rows_copy(3, 3, 7, 5)
    own_to_a = rows_copy(4, 0, 7, 7)
    diag_to_partner = rows_copy(5, 5, 1, 4)
    a_to_partner = rows_copy(6, 7, 1, 6)

    def gate_copy(k):
        ep, _ = place(k)
        return remote(gt_hbm.at[pl.ds(pl.multiple_of(ep * n_loc, n_loc), n_loc), :], g_buf.at[MIRROR[k]], g_send.at[k], g_recv.at[MIRROR[k]], k)

    def dg_copy(k):
        return remote(dgt_s.at[k % 2], dg_recv.at[my_blk], dg_send.at[k], dg_rsem.at[MIRROR[k]], k)

    def tok_copy(k):
        src = tok_s.at[k % 2]
        if k % 2 == 0:
            i = (k - 2) // 2
            return remote(src, pair_s.at[i % 2], tok_send.at[k], pair_rsem.at[i], 1)
        i = (k - 1) // 2
        return remote(src, tok_recv.at[i], tok_send.at[k], tok_rsem.at[i], k)

    own_tok = pltpu.make_async_copy(tok_s.at[0], tok_own, own_sem.at[0])
    own_dg = pltpu.make_async_copy(dgt_s.at[0], dg_recv.at[my_blk], own_sem.at[1])

    def loads(c, slot):
        return [pltpu.make_async_copy(h_buf.at[c], h_s.at[slot], in_sem.at[slot, 0]),
                pltpu.make_async_copy(dy_buf.at[c], dy_s.at[slot], in_sem.at[slot, 1]),
                pltpu.make_async_copy(g_buf.at[c], gt_s.at[slot, pl.ds(0, n_loc), :], in_sem.at[slot, 2])]

    def own_loads():
        return [pltpu.make_async_copy(h_hbm, h_s.at[0], in_sem.at[0, 0]),
                pltpu.make_async_copy(dy_hbm, dy_s.at[0], in_sem.at[0, 1]),
                pltpu.make_async_copy(gt_hbm.at[pl.ds(pl.multiple_of(my_ep * n_loc, n_loc), n_loc), :],
                                      gt_s.at[0, pl.ds(0, n_loc), :], in_sem.at[0, 2])]

    def w_loads(e):
        return [pltpu.make_async_copy(wg_hbm.at[e], wgu.at[e, :, pl.ds(0, half)], w_sem.at[e, 0]),
                pltpu.make_async_copy(wu_hbm.at[e], wgu.at[e, :, pl.ds(half, half)], w_sem.at[e, 1]),
                pltpu.make_async_copy(wd_hbm.at[e], wd.at[e], w_sem.at[e, 2])]

    def dw_stores(e):
        return [pltpu.make_async_copy(dwgu.at[e, :, pl.ds(0, half)], dwg_hbm.at[e], dw_sem.at[e, 0]),
                pltpu.make_async_copy(dwgu.at[e, :, pl.ds(half, half)], dwu_hbm.at[e], dw_sem.at[e, 1]),
                pltpu.make_async_copy(dwd.at[e], dwd_hbm.at[e], dw_sem.at[e, 2])]

    def start(copies):
        for cp in copies:
            cp.start()

    def wait_recv(copies):
        for cp in copies:
            cp.wait_recv()

    gt_s[...] = jnp.zeros_like(gt_s)
    start(own_to_b)
    start(own_to_partner)
    start(own_loads())
    for k in range(1, n_blk):
        gate_copy(k).start()

    def start_w(e, _):
        start(w_loads(e))
        return 0
    lax.fori_loop(0, n_loc, start_w, 0)

    arrivals = {1: own_to_partner, 2: b_to_partner, 4: diag_to_partner, 6: a_to_partner}

    def block(s, _):
        slot = s % 2
        for cp in loads(s, slot):
            cp.wait()
        h_ref, dy_ref = h_s.at[slot], dy_s.at[slot]
        g_s[...] = gt_s[slot].T
        ht_s[...] = h_ref[...].T
        out_acc[...] = jnp.zeros_like(out_acc)
        dh_acc[...] = jnp.zeros_like(dh_acc)
        dg_acc[...] = jnp.zeros_like(dg_acc)

        def expert(e, _):
            @pl.when(s == 0)
            def _():
                for cp in w_loads(e):
                    cp.wait()
                dwgu[e] = jnp.zeros(dwgu.shape[1:], F32)
                dwd[e] = jnp.zeros(dwd.shape[1:], F32)

            @pl.when(jnp.logical_and(s == 1, e == 1))
            def _():
                wait_recv(own_to_b)
                start(b_to_partner)
                start(b_to_a)
                start(own_to_a)

            @pl.when(jnp.logical_and(s == 3, e == 0))
            def _():
                wait_recv(b_to_a)
                start(diag_to_partner)

            @pl.when(jnp.logical_and(s == 3, e == 4))
            def _():
                wait_recv(own_to_a)
                start(a_to_partner)

            for k in range(n_blk - 1):
                @pl.when(jnp.logical_and(s == k, e == n_loc - 1))
                def _():
                    if k + 1 in arrivals:
                        wait_recv(arrivals[k + 1])
                    gate_copy(MIRROR[k + 1]).wait_recv()
                    start(loads(k + 1, (k + 1) % 2))

            expert_step(e, None, h_ref, ht_s, dy_ref, g_s, wgu, wd, dwgu, dwd, out_acc, dh_acc, dg_acc)

            @pl.when(s == n_blk - 1)
            def _():
                start(dw_stores(e))
            return 0
        lax.fori_loop(0, n_loc, expert, 0)

        for k in range(2, n_blk):
            @pl.when(s == k)
            def _():
                if k == 2:
                    own_tok.wait()
                    own_dg.wait()
                else:
                    tok_copy(k - 2).wait_send()
                    dg_copy(k - 2).wait_send()
        tile = rows // 8
        is_pair = jnp.logical_and(s % 2 == 1, s > 1)

        @pl.when(is_pair)
        def _():
            for k in (3, 5, 7):
                @pl.when(s == k)
                def _():
                    tok_copy(k - 1).wait_recv()
            side = ((s - 3) // 2) % 2

            def fold(i, _):
                r = pl.ds(pl.multiple_of(i * tile, tile), tile)
                tok_s[slot, r, pl.ds(0, d)] = (out_acc[r, :] + pair_s[side, r, pl.ds(0, d)].astype(F32)).astype(BF16)
                tok_s[slot, r, pl.ds(d, d)] = (dh_acc[r, :] + pair_s[side, r, pl.ds(d, d)].astype(F32)).astype(BF16)
                return 0
            lax.fori_loop(0, 8, fold, 0)

        @pl.when(jnp.logical_not(is_pair))
        def _():
            def keep(i, _):
                r = pl.ds(pl.multiple_of(i * tile, tile), tile)
                tok_s[slot, r, pl.ds(0, d)] = out_acc[r, :].astype(BF16)
                tok_s[slot, r, pl.ds(d, d)] = dh_acc[r, :].astype(BF16)
                return 0
            lax.fori_loop(0, 8, keep, 0)
        dgt_s[slot] = dg_acc[...].T[:n_loc]
        for k in range(n_blk):
            @pl.when(s == k)
            def _():
                if k == 0:
                    own_tok.start()
                    own_dg.start()
                else:
                    tok_copy(k).start()
                    dg_copy(k).start()
        return 0

    lax.fori_loop(0, n_blk, block, 0)

    for k in (6, 7):
        tok_copy(k).wait_send()
        dg_copy(k).wait_send()
    for k in (1, 3, 5, 7):
        tok_copy(k).wait_recv()
    for k in range(1, n_blk):
        dg_copy(MIRROR[k]).wait_recv()
        gate_copy(k).wait_send()
    for copies in (own_to_partner, own_to_b, b_to_partner, b_to_a, own_to_a, diag_to_partner, a_to_partner):
        for cp in copies:
            cp.wait_send()

    def end_w(e, _):
        for cp in dw_stores(e):
            cp.wait()
        return 0
    lax.fori_loop(0, n_loc, end_w, 0)


def dense_experts(hidden, dy, gates_t, w_gate, w_up, w_down):
    rows, d = hidden.shape
    n_loc, _, half = w_gate.shape
    n_blk = len(FLIPS)
    flops = 18 * n_blk * rows * n_loc * d * half
    dma = pltpu.SemaphoreType.DMA
    out = pl.pallas_call(
        dense_kernel,
        out_shape=[jax.ShapeDtypeStruct((rows, 2 * d), BF16),
                   jax.ShapeDtypeStruct((4, rows, 2 * d), BF16),
                   jax.ShapeDtypeStruct((n_blk, n_loc, rows), F32),
                   jax.ShapeDtypeStruct((n_blk, rows, d), BF16),
                   jax.ShapeDtypeStruct((n_blk, rows, d), BF16),
                   jax.ShapeDtypeStruct((n_blk, n_loc, rows), F32),
                   jax.ShapeDtypeStruct(w_gate.shape, F32),
                   jax.ShapeDtypeStruct(w_up.shape, F32),
                   jax.ShapeDtypeStruct(w_down.shape, F32)],
        in_specs=[pl.BlockSpec(memory_space=pl.ANY)] * 6,
        out_specs=[pl.BlockSpec(memory_space=pl.ANY)] * 9,
        scratch_shapes=[
            pltpu.VMEM((2, rows, d), BF16), pltpu.VMEM((2, rows, d), BF16),
            pltpu.VMEM((2, 128, rows), F32), pltpu.VMEM((rows, 128), F32),
            pltpu.VMEM((d, rows), BF16),
            pltpu.VMEM((n_loc, d, 2 * half), BF16), pltpu.VMEM((n_loc, half, d), BF16),
            pltpu.VMEM((n_loc, d, 2 * half), F32), pltpu.VMEM((n_loc, half, d), F32),
            pltpu.VMEM((rows, d), F32), pltpu.VMEM((rows, d), F32), pltpu.VMEM((rows, 128), F32),
            pltpu.VMEM((2, rows, 2 * d), BF16), pltpu.VMEM((2, n_loc, rows), F32),
            pltpu.VMEM((2, rows, 2 * d), BF16),
            dma((2, 3)), dma((n_loc, 3)), dma((n_loc, 3)),
            dma((7, 2)), dma((n_blk, 2)), dma((n_blk,)), dma((n_blk,)),
            dma((n_blk,)), dma((4,)), dma((3,)), dma((n_blk,)), dma((n_blk,)), dma((2,)),
        ],
        compiler_params=pltpu.CompilerParams(vmem_limit_bytes=67_000_000, has_side_effects=True),
        cost_estimate=pl.CostEstimate(flops=flops, bytes_accessed=100_000_000, transcendentals=0),
        name="dense_experts",
    )(hidden, dy, gates_t, w_gate, w_up, w_down)
    return out[0], out[1], out[2], out[6], out[7], out[8]


def solution(mesh):
    tok_spec = P(("dp", "ep", "tp"), None)
    wide_spec = P("ep", None, "tp")
    down_spec = P("ep", "tp", None)
    grad_wide = P(("dp", "ep"), None, "tp")
    grad_down = P(("dp", "ep"), "tp", None)

    def device_step(x_in, norm_gain, w_router, expert_idx, w_gate, w_up, w_down, out_bias, dy_out):
        n_tok, d = x_in.shape
        n_exp = w_router.shape[1]
        n_loc = w_gate.shape[0]
        group = ("ep", "tp")
        x_f32 = x_in.astype(F32)
        inv_rms = lax.rsqrt(jnp.mean(x_f32 * x_f32, axis=-1, keepdims=True) + EPS)
        normed = x_f32 * inv_rms
        gain = norm_gain.astype(F32)
        hidden = (normed * gain).astype(BF16)
        logits = jnp.dot(hidden, w_router, preferred_element_type=F32)
        chosen = jnp.any(expert_idx[:, :, None] == jnp.arange(n_exp)[None, None, :], axis=1)
        gates = jax.nn.softmax(jnp.where(chosen, logits, -jnp.inf), axis=-1)
        tok_own, tok_recv, dg, d_gate, d_up, d_down = dense_experts(hidden, dy_out, gates.T, w_gate, w_up, w_down)
        tok = tok_own.astype(F32) + jnp.sum(tok_recv.astype(F32), axis=0)
        d_gates = jnp.sum(dg.reshape(-1, 2, n_loc, n_tok), axis=1).reshape(n_exp, n_tok).T
        moe_out = tok[:, :d] + out_bias.astype(F32)
        y_out = (x_f32 + moe_out).astype(BF16)
        dy_f32 = dy_out.astype(F32)
        d_bias = jnp.sum(dy_f32, axis=0)
        d_logits = gates * (d_gates - jnp.sum(gates * d_gates, axis=-1, keepdims=True))
        d_router = jnp.einsum("td,te->de", hidden, d_logits, preferred_element_type=F32)
        dh_total = tok[:, d:] + jnp.einsum("te,de->td", d_logits, w_router, preferred_element_type=F32)
        d_gain = jnp.sum(dh_total * normed, axis=0)
        d_norm = dh_total * gain
        dx_in = (dy_f32 + inv_rms * (d_norm - normed * jnp.mean(d_norm * normed, axis=-1, keepdims=True))).astype(BF16)
        sums = lax.psum(jnp.concatenate([d_router.T, d_gain[None], d_bias[None]], axis=0), group)
        d_router, d_gain, d_bias = sums[:n_exp].T, sums[n_exp], sums[n_exp + 1]
        return y_out, dx_in, d_gain, d_router, d_gate, d_up, d_down, d_bias

    return jax.shard_map(device_step, mesh=mesh, in_specs=(tok_spec, P(None), P(None, None), tok_spec, wide_spec, wide_spec, down_spec, P(None), tok_spec), out_specs=(tok_spec, tok_spec, P("dp"), P("dp", None), grad_wide, grad_wide, grad_down, P("dp")), check_vma=False)
```

time: 473 us -> 331 us (0.70)
  waiting for transfers between devices: 200 us -> 42.5 us
  blocking collectives: 41.1 us -> 0 us
  Pallas kernels: 196 us -> 230 us
  local copies, waits for them, and re-layouts: 9.44 us -> 24.5 us
  other arithmetic: 7.27 us -> 16.5 us
    reduce_scatter x1 -> x0, waiting for transfers between devices: 96.1 us -> none  [device_step(): lax.psum_scatter(tok.reshape(-1, 2 * d), group, scatter_dimension=0, tile...]
    all_gather x2 -> x0, waiting for transfers between devices: 79.5 us -> none  [the longest x1 50.2 us: device_step(): dy_all = lax.all_gather(dy_out, group, axis=0)]
    pallas_call x1, Pallas kernels: 196 us -> 230 us  [dense_experts(): pl.pallas_call(dense_kernel, out_shape=[jax.ShapeDtypeStruct((rows, 2 * d...]
    psum x1, waiting for transfers between devices: 18.7 us -> 42.5 us  [device_step(): lax.psum(jnp.concatenate([d_router.T, d_gain[None], d_bias[None]], axis=0...]
    psum x1 -> x0, blocking collectives: 22.3 us -> none  [device_step(): d_gain, d_router, d_bias = lax.psum((d_gain, d_router, d_bias), group)]
    all_gather x1 -> x0, blocking collectives: 18.8 us -> none  [device_step(): g_all = lax.all_gather(gates, group, axis=0)]
    unnamed x41, local copies, waits for them, and re-layouts: 3.73 us -> 21.5 us
    reduce_sum x1 -> x2, other arithmetic: 0.01 us -> 6.73 us  [the longest x1 5.81 us: device_step(): tok = tok_own.astype(F32) + jnp.sum(tok_recv.astype(F32), axis=0)]
  transfers between devices with their start and end apart: 5 -> 1, of which waited for: 5 -> 1; matrix products, arithmetic and copies ran while one was open for 3% -> 0% of each run, Pallas kernels for 0% -> 0%
where the time goes in v2:
time: 331 us
  Pallas kernels  230 us (69%)
  waiting for transfers between devices  42.5 us (13%)
  local copies, waits for them, and re-layouts  24.5 us (7%)
  other arithmetic  16.5 us (5%)
  between operations  14.2 us (4%)
    pallas_call x1, Pallas kernels, dense_experts(): pl.pallas_call(dense_kernel, out_shape=[jax.ShapeDtypeStruct((rows, 2 * d...  230 us
    psum x1, waiting for transfers between devices, device_step(): lax.psum(jnp.concatenate([d_router.T, d_gain[None], d_bias[None]], axis=0...  42.5 us
    unnamed x41, local copies, waits for them, and re-layouts  21.5 us
  transfers between devices with their start and end apart: 1, of which 1 were waited for; matrix products, arithmetic and copies ran while one was open for 0% of the time, Pallas kernels for 0%

profile of v2, /device:TPU:0, one launch (start us, length us, event | category | flops | bytes accessed | tf_op | source)
XLA Modules:
  0.0 330.6 jit_solution(8137166018175095851)
XLA Ops:
  7.2 0.0 copy-start.6
  7.2 0.0 all-reduce.2.cloned.1.call-start
  7.2 1.5 fusion.10
  8.7 0.0 copy-start.14
  8.8 0.7 convert_element_type.28
  9.4 0.8 fusion.12
  10.2 1.5 fusion.5.h_hbm
  11.8 1.0 copy-done.1
  12.7 0.4 fusion.24
  13.2 0.0 copy-start.2
  13.2 0.0 copy-start.8
  13.3 0.6 copy-done.2
  13.8 0.6 copy-done.12
  14.4 0.6 fusion.22.gt_hbm
  15.1 230.0 %dense_experts.1 = (bf16[512,2048]{1,0:T(8,128)(2,1)}, bf16[4,512,2048]{2,1,0:T(8,128)(2,1)}, f32[8,8,512]{2,1,0:T(8,128)}, bf16[8,512,1024]{2,1,0:T(8,128)(2,1)...) custom-call(bf16[512,1024]{1,0:T(8,128)(2,1)} %copy-done.1, ...), custom_call_target="tpu_custom_call" | custom-call | flops 154618822656 | bytes 100000000 | tf_op jit(solution)/shard_map/dense_experts/pallas_call | solution.py:287
  245.1 0.9 bitcast_reduce_fusion
  246.0 0.9 fusion.13
  246.9 1.5 fusion.17
  248.4 5.8 %convert_reduce_fusion = f32[512,2048]{1,0:T(8,128)S(1)} fusion(bf16[4,512,2048]{2,1,0:T(8,128)(2,1)} %get-tuple-element.15), kind=kLoop, calls=%fused_computation | loop fusion | flops 7340032 | bytes 12582912 | tf_op jit(solution)/shard_map/reduce_sum | solution.py:341
  254.3 0.6 convert_add_fusion
  254.9 0.6 copy-done
  255.5 0.9 fusion.9
  256.4 0.3 copy-done.5
  256.7 2.4 convert_reduce_fusion.1
  259.1 0.7 pad_maximum_fusion
  259.8 0.0 all-reduce.2.cloned.1.call-update
  259.8 42.5 %all-reduce.2.cloned.1.call-done = f32[34,1024]{1,0:T(8,128)} async-done(((f32[34,1024]{1,0:T(8,128)}), f32[34,1024]{1,0:T(8,128)}) %all-reduce.2.cloned.1.call-update) | async-done | bytes 139280 | tf_op jit(solution)/shard_map/psum | solution.py:353
  302.4 1.6 slice_bitcast_fusion
  303.9 1.4 fusion.23
  305.4 7.5 %copy.22 = f32[8,1024,256]{2,1,0:T(8,128)} copy(f32[8,1024,256]{2,1,0:T(8,128)} %get-tuple-element.42) | data formatting | bytes 16777216
  312.9 7.5 %copy.23 = f32[8,1024,256]{2,1,0:T(8,128)} copy(f32[8,1024,256]{2,1,0:T(8,128)} %get-tuple-element.43) | data formatting | bytes 16777216
  320.4 3.4 %copy.24 = f32[8,256,1024]{2,1,0:T(8,128)} copy(f32[8,256,1024]{2,1,0:T(8,128)S(1)} %bitcast.28) | data formatting | bytes 16777216
  (34 shorter events, 0.1 us)
Async XLA Ops:
  7.2 5.6 %copy-start.6 = (bf16[1024,32]{0,1:T(8,128)(2,1)S(1)}, bf16[1024,32]{0,1:T(8,128)(2,1)}, u32[]{:S(2)}) copy-start(bf16[1024,32]{0,1:T(8,128)(2,1)} %param.11) | copy-start | bytes 196612
  7.2 295.2 %all-reduce.2.cloned.1.call-start = ((), (), s32[]{:S(2)}) async-start(), calls=%async_computation | async-start | bytes 327680 | tf_op jit(solution)/shard_map/psum | solution.py:353
  8.7 4.5 %copy-start.14 = (f32[512]{0:T(512)}, f32[512]{0:T(512)S(1)}, u32[]{:S(2)}) copy-start(f32[512]{0:T(512)S(1)} %add_rsqrt_fusion) | copy-start | bytes 6148
  9.4 3.8 %copy-start.10 = (f32[1024]{0:T(1024)}, f32[1024]{0:T(1024)S(1)}, u32[]{:S(2)}) copy-start(f32[1024]{0:T(1024)S(1)} %convert_element_type.28) | copy-start | bytes 12292
  11.8 1.0 copy-start.1
  13.2 0.6 copy-start.2
  13.2 0.6 copy-start.8
  13.8 0.6 copy-start.12
  15.1 231.0 %copy-start.9 = (f32[512]{0:T(512)S(1)}, f32[512]{0:T(512)}, u32[]{:S(2)}) copy-start(f32[512]{0:T(512)} %copy-done.8) | copy-start | bytes 6148
  15.1 231.0 %copy-start.13 = (f32[512]{0:T(512)S(1)}, f32[512]{0:T(512)}, u32[]{:S(2)}) copy-start(f32[512]{0:T(512)} %copy-done.12) | copy-start | bytes 6148
  248.4 5.8 %copy-start.4 = (bf16[512,2048]{1,0:T(8,128)(2,1)S(1)}, bf16[512,2048]{1,0:T(8,128)(2,1)}, u32[]{:S(2)}) copy-start(bf16[512,2048]{1,0:T(8,128)(2,1)} %get-tuple-element.14) | copy-start | bytes 6291460
  254.3 1.2 copy-start
  254.3 1.2 copy-start.3
  254.3 1.2 copy-start.7
  254.3 1.2 copy-start.11
  254.3 1.2 copy-start.15
  255.5 0.9 copy-start.16
  255.5 1.2 copy-start.5
  305.4 15.0 %slice-start = ((s8[8388608]{0:T(1024)(128)(4,1)}), s8[4194304]{0:T(1024)(128)(4,1)S(1)}, s32[]{:S(2)}) async-start(s8[8388608]{0:T(1024)(128)(4,1)} %bitcast.27), calls=%async_computation.1 | async-start | bytes 8388608
  312.9 7.5 %slice-start.1 = ((s8[8388608]{0:T(1024)(128)(4,1)}), s8[4194304]{0:T(1024)(128)(4,1)S(1)}, s32[]{:S(2)}) async-start(s8[8388608]{0:T(1024)(128)(4,1)} %bitcast.27), calls=%async_computation.2 | async-start | bytes 8388608
Sparse Core Ops, SparseCore 0:
  260.0 42.3 all-reduce.1
